TPU v7x, 32 devices: a whole 2x2x4 slice. The times are simulated.
32 devices in a mesh: seq: 8 (over z, y), grp: 4 (over x, core).
Axes of the slice: x: 2, y: 2, z: 4, core: 2. Of those that a mesh axis runs over, the one named last changes fastest.
Arguments:
- hidden: bfloat16 [4096, 2048], P('seq', 'grp'), may hold values from -8 to 8
- qkv_weight: bfloat16 [3, 2048, 6144], P(None, 'seq', 'grp'), may hold values from -0.125 to 0.125
- out_weight: bfloat16 [3, 2048, 2048], P(None, 'grp', 'seq'), may hold values from -0.125 to 0.125
- projection: float32 [3, 16, 128, 128], P(None, 'grp'), may hold values from -6 to 6
- norm_gain: float32 [3, 2048], replicated, may hold values from 0.1 to 1.9
- out_gain: float32 [3, 2048], P(None, 'grp'), may hold values from 0.1 to 1.9
Outputs:
- layer_out: bfloat16 [4096, 2048], P('seq', 'grp')
All inputs are finite; a program needn't handle non-finite values.
Results may differ from a plain program's by a relative error of at most 0.034.
Values may be sent and summed in bfloat16 or wider, within the bound.
A program may use at most 64 MiB of HBM per device.

v0:
```python
import math
import jax
import jax.numpy as jnp
from jax import lax
from jax.sharding import PartitionSpec as P

stabilizer = 2.0
highest = lax.Precision.HIGHEST


def prefix(array, axis, combine, identity):
    peers, index = (lax.axis_size(axis), lax.axis_index(axis))
    everything = jax.tree.map(
        lambda part, kind: lax.all_gather(part.astype(kind), axis),
        array,
        (jnp.bfloat16, jnp.bfloat16),
    )
    start = jax.tree.map(
        lambda part, zero: jnp.broadcast_to(jnp.asarray(zero, part.dtype), part.shape),
        array,
        identity,
    )

    def step(k, before):
        reached = k < index
        new = combine(
            before, jax.tree.map(lambda part, own: part[k].astype(own.dtype), everything, array)
        )
        return jax.tree.map(lambda a, b: jnp.where(reached, a, b), new, before)

    return lax.fori_loop(0, peers, step, start)


def features(rows, projection_layer):
    head_size = rows.shape[-1]
    feature_count = projection_layer.shape[-1]
    scaled = rows.astype(jnp.float32) * head_size ** (-0.25)
    mixed = jnp.einsum("thd,hdm->thm", scaled, projection_layer, precision=highest)
    energy = 0.5 * jnp.sum(scaled * scaled, axis=-1, keepdims=True)
    return (jnp.exp(mixed - energy - stabilizer) / math.sqrt(feature_count)).astype(jnp.bfloat16)


def add_states(earlier, later):
    return (earlier[0] + later[0], earlier[1] + later[1])


def local(hidden, qkv_weight, out_weight, projection, norm_gain, out_gain):
    layer_count = qkv_weight.shape[0]
    local_heads = projection.shape[1]
    head_size = projection.shape[2]
    feature_count = projection.shape[3]
    token_rows = hidden.shape[0]
    stream = hidden
    causal_mask = jnp.arange(token_rows)[:, None] >= jnp.arange(token_rows)[None, :]
    for layer_index in range(layer_count):
        gathered = lax.all_gather(stream, "grp", axis=1, tiled=True)
        wide = gathered.astype(jnp.float32)
        inverse_rms = lax.rsqrt(jnp.mean(wide * wide, axis=-1, keepdims=True) + 1e-05)
        normed = (wide * inverse_rms * norm_gain[layer_index][None, :]).astype(jnp.bfloat16)
        qkv_wide = jnp.dot(
            normed,
            lax.all_gather(qkv_weight[layer_index], "seq", axis=0, tiled=True),
            preferred_element_type=jnp.float32,
        )
        qkv = qkv_wide.astype(jnp.bfloat16).reshape(token_rows, local_heads, 3, head_size)
        query_feat = features(qkv[:, :, 0], projection[layer_index])
        key_feat = features(qkv[:, :, 1], projection[layer_index])
        value_rows = qkv[:, :, 2]
        block_kv = jnp.einsum(
            "jhm,jhe->hme", key_feat, value_rows, preferred_element_type=jnp.float32
        )
        block_z = jnp.sum(key_feat.astype(jnp.float32), axis=0)
        zero_kv = jnp.zeros((local_heads, feature_count, head_size), jnp.float32)
        zero_z = jnp.zeros((local_heads, feature_count), jnp.float32)
        prefix_kv, prefix_z = prefix((block_kv, block_z), "seq", add_states, (zero_kv, zero_z))
        scores = jnp.einsum(
            "ihm,jhm->hij", query_feat, key_feat, preferred_element_type=jnp.float32
        )
        masked = jnp.where(causal_mask[None], scores, jnp.zeros_like(scores))
        score_weights = masked.astype(jnp.bfloat16)
        query_wide = query_feat.astype(jnp.float32)
        denominator = jnp.sum(masked, axis=-1) + jnp.einsum(
            "ihm,hm->hi", query_wide, prefix_z, precision=highest
        )
        numerator = jnp.einsum(
            "hij,jhe->hie", score_weights, value_rows, preferred_element_type=jnp.float32
        )
        numerator = numerator + jnp.einsum(
            "ihm,hme->hie",
            query_feat,
            prefix_kv.astype(jnp.bfloat16),
            preferred_element_type=jnp.float32,
        )
        attention = numerator / denominator[..., None]
        inverse_norm = lax.rsqrt(jnp.mean(attention * attention, axis=-1, keepdims=True) + 1e-06)
        head_gain = out_gain[layer_index].reshape(local_heads, head_size)[:, None, :]
        attended = (attention * inverse_norm * head_gain).astype(jnp.bfloat16)
        attended = jnp.transpose(attended, (1, 0, 2)).reshape(token_rows, local_heads * head_size)
        terms = jnp.dot(
            attended,
            lax.all_gather(out_weight[layer_index], "seq", axis=1, tiled=True),
            preferred_element_type=jnp.float32,
        )
        summed = lax.psum_scatter(
            terms.astype(jnp.bfloat16), "grp", scatter_dimension=1, tiled=True
        ).astype(jnp.float32)
        stream = (stream.astype(jnp.float32) + summed).astype(jnp.bfloat16)
    return stream


def solution(mesh):
    return jax.shard_map(
        local,
        mesh=mesh,
        in_specs=(
            P("seq", "grp"),
            P(None, "seq", "grp"),
            P(None, "grp", "seq"),
            P(None, "grp", None, None),
            P(),
            P(None, "grp"),
        ),
        out_specs=P("seq", "grp"),
        check_vma=False,
    )
```

profile of v0, /device:TPU:0, one launch (start us, length us, event | category | flops | bytes accessed | tf_op | source)
XLA Modules:
  0.0 804.3 jit_solution(3640511315558074532)
XLA Ops:
  7.3 3.1 fusion.132
  10.6 23.6 %all-gather.28.cloned.1.call-done = bf16[512,2048]{1,0:T(8,128)(2,1)} async-done(((bf16[512,512]{1,0:T(8,128)(2,1)}), bf16[512,2048]{1,0:T(8,128)(2,1)}) %all-gather.28.cloned.1.call-update) | async-done | bytes 2097168 | tf_op jit(solution)/shard_map/all_gather | solution.py:56
  34.2 2.2 fusion.6
  36.4 98.7 %all-gather.34.cloned.1.call-done = bf16[1,2048,1536]{2,1,0:T(8,128)(2,1)} async-done(((bf16[1,256,1536]{2,1,0:T(8,128)(2,1)}), bf16[1,2048,1536]{2,1,0:T(8,128)(2,1)}) %all-gather.34.cloned.1.call-update) | async-done | bytes 6291472 | tf_op jit(solution)/shard_map/all_gather | solution.py:62
  135.1 7.4 fusion.15
  142.6 1.7 copy.46
  145.0 2.3 fusion.139
  148.3 2.0 fusion.136
  151.3 17.7 %all-gather.12 = bf16[8,4,128]{2,1,0:T(4,128)(2,1)S(1)} all-gather(bf16[1,4,128]{2,1,0:T(4,128)(2,1)S(1)} %bitcast.327), channel_id=4, replica_groups=mesh['seq'=8,'grp'=4] {'seq'}, dimensions={0}, use_global_device_ids=true | all-gather | bytes 9216 | tf_op jit(solution)/shard_map/all_gather | solution.py:14
  169.6 2.2 fusion.77
  171.9 2.1 select_reduce_fusion.2
  174.0 13.0 %all-gather.36.cloned.1.call-done = bf16[32,128,128]{2,1,0:T(8,128)(2,1)} async-done(((bf16[4,128,128]{2,1,0:T(8,128)(2,1)}), bf16[32,128,128]{2,1,0:T(8,128)(2,1)}) %all-gather.36.cloned.1.call-update) | async-done | bytes 1048592 | tf_op jit(solution)/shard_map/all_gather | solution.py:14
  186.9 8.7 %while.48 = (s32[]{:T(128)}, f32[4,128,128]{2,1,0:T(8,128)S(1)}, f32[4,128]{1,0:T(4,128)S(1)}, s32[]{:T(128)}, bf16[8,4,128,128]{3,2,1,0:T(8,128)(2,1)}, /*index...) while((s32[]{:T(128)}, f32[4,128,128]{2,1,0:T(8,128)S(1)}, f32[4,128]{1,0:T(4,128)S(1)}, ...), condition=%wide.region_5.6_spmd.clone, body=%wide.region_4.5_spmd.clone.sunk | while | flops 264196 | bytes 660595 | solution.py:31
  186.9 1.1 add_select_fusion.12
  188.0 1.0 add_select_fusion.12
  190.2 1.0 add_select_fusion.12
  191.3 1.0 add_select_fusion.12
  192.4 1.0 add_select_fusion.12
  193.5 1.0 add_select_fusion.12
  194.5 1.0 add_select_fusion.12
  198.1 39.8 %all-gather.38.cloned.1.call-done = bf16[1,512,2048]{2,1,0:T(8,128)(2,1)} async-done(((bf16[1,512,256]{2,1,0:T(8,128)(2,1)}), bf16[1,512,2048]{2,1,0:T(8,128)(2,1)}) %all-gather.38.cloned.1.call-update) | async-done | bytes 2097168 | tf_op jit(solution)/shard_map/all_gather | solution.py:101
  237.9 4.2 convolution_convert_fusion.2
  242.2 29.4 %reduce-scatter.4.cloned.1.call-done = bf16[512,512]{1,0:T(8,128)(2,1)} async-done(((bf16[512,2048]{1,0:T(8,128)(2,1)}), bf16[512,512]{1,0:T(8,128)(2,1)}) %reduce-scatter.4.cloned.1.call-update) | async-done | bytes 524304 | tf_op jit(solution)/shard_map/reduce_scatter | solution.py:104
  271.6 2.0 add_convert_fusion.2
  274.6 21.8 %all-gather.30.cloned.1.call-done = bf16[512,2048]{1,0:T(8,128)(2,1)} async-done(((bf16[512,512]{1,0:T(8,128)(2,1)}), bf16[512,2048]{1,0:T(8,128)(2,1)}) %all-gather.30.cloned.1.call-update) | async-done | bytes 2097168 | tf_op jit(solution)/shard_map/all_gather | solution.py:56
  296.3 2.2 fusion.9
  298.6 98.7 %all-gather.40.cloned.1.call-done = bf16[1,2048,1536]{2,1,0:T(8,128)(2,1)} async-done(((bf16[1,256,1536]{2,1,0:T(8,128)(2,1)}), bf16[1,2048,1536]{2,1,0:T(8,128)(2,1)}) %all-gather.40.cloned.1.call-update) | async-done | bytes 6291472 | tf_op jit(solution)/shard_map/all_gather | solution.py:62
  397.3 7.4 fusion.18
  404.7 1.7 copy.54
  407.1 2.2 fusion.140
  411.2 17.7 %all-gather.13 = bf16[8,4,128]{2,1,0:T(4,128)(2,1)S(1)} all-gather(bf16[1,4,128]{2,1,0:T(4,128)(2,1)S(1)} %bitcast.329), channel_id=8, replica_groups=mesh['seq'=8,'grp'=4] {'seq'}, dimensions={0}, use_global_device_ids=true | all-gather | bytes 9216 | tf_op jit(solution)/shard_map/all_gather | solution.py:14
  429.6 2.2 fusion.75
  431.8 2.1 select_reduce_fusion.1
  433.9 15.0 %all-gather.42.cloned.1.call-done = bf16[32,128,128]{2,1,0:T(8,128)(2,1)} async-done(((bf16[4,128,128]{2,1,0:T(8,128)(2,1)}), bf16[32,128,128]{2,1,0:T(8,128)(2,1)}) %all-gather.42.cloned.1.call-update) | async-done | bytes 1048592 | tf_op jit(solution)/shard_map/all_gather | solution.py:14
  449.0 8.7 %while.49 = (s32[]{:T(128)}, f32[4,128,128]{2,1,0:T(8,128)S(1)}, f32[4,128]{1,0:T(4,128)S(1)}, s32[]{:T(128)}, bf16[8,4,128,128]{3,2,1,0:T(8,128)(2,1)}, /*index...) while((s32[]{:T(128)}, f32[4,128,128]{2,1,0:T(8,128)S(1)}, f32[4,128]{1,0:T(4,128)S(1)}, ...), condition=%wide.region_14.15_spmd.clone, body=%wide.region_13.14_spmd.clone.sunk | while | flops 264196 | bytes 660595 | solution.py:31
  449.0 1.1 add_select_fusion.14
  450.1 1.0 add_select_fusion.14
  451.2 1.0 add_select_fusion.14
  452.2 1.0 add_select_fusion.14
  454.4 1.0 add_select_fusion.14
  455.5 1.0 add_select_fusion.14
  456.6 1.0 add_select_fusion.14
  460.1 40.0 %all-gather.44.cloned.1.call-done = bf16[1,512,2048]{2,1,0:T(8,128)(2,1)} async-done(((bf16[1,512,256]{2,1,0:T(8,128)(2,1)}), bf16[1,512,2048]{2,1,0:T(8,128)(2,1)}) %all-gather.44.cloned.1.call-update) | async-done | bytes 2097168 | tf_op jit(solution)/shard_map/all_gather | solution.py:101
  500.1 4.2 convolution_convert_fusion.1
  504.4 29.4 %reduce-scatter.6.cloned.1.call-done = bf16[512,512]{1,0:T(8,128)(2,1)} async-done(((bf16[512,2048]{1,0:T(8,128)(2,1)}), bf16[512,512]{1,0:T(8,128)(2,1)}) %reduce-scatter.6.cloned.1.call-update) | async-done | bytes 524304 | tf_op jit(solution)/shard_map/reduce_scatter | solution.py:104
  533.8 2.0 add_convert_fusion.1
  536.7 21.9 %all-gather.32.cloned.1.call-done = bf16[512,2048]{1,0:T(8,128)(2,1)} async-done(((bf16[512,512]{1,0:T(8,128)(2,1)}), bf16[512,2048]{1,0:T(8,128)(2,1)}) %all-gather.32.cloned.1.call-update) | async-done | bytes 2097168 | tf_op jit(solution)/shard_map/all_gather | solution.py:56
  558.6 2.2 fusion.12
  560.8 98.5 %all-gather.46.cloned.1.call-done = bf16[1,2048,1536]{2,1,0:T(8,128)(2,1)} async-done(((bf16[1,256,1536]{2,1,0:T(8,128)(2,1)}), bf16[1,2048,1536]{2,1,0:T(8,128)(2,1)}) %all-gather.46.cloned.1.call-update) | async-done | bytes 6291472 | tf_op jit(solution)/shard_map/all_gather | solution.py:62
  659.3 7.4 fusion.21
  666.7 1.7 copy.62
  669.2 2.3 fusion.141
  673.1 17.7 %all-gather.14 = bf16[8,4,128]{2,1,0:T(4,128)(2,1)S(1)} all-gather(bf16[1,4,128]{2,1,0:T(4,128)(2,1)S(1)} %bitcast.328), channel_id=12, replica_groups=mesh['seq'=8,'grp'=4] {'seq'}, dimensions={0}, use_global_device_ids=true | all-gather | bytes 9216 | tf_op jit(solution)/shard_map/all_gather | solution.py:14
  691.5 2.2 fusion.73
  693.7 2.1 select_reduce_fusion
  695.8 15.3 %all-gather.48.cloned.1.call-done = bf16[32,128,128]{2,1,0:T(8,128)(2,1)} async-done(((bf16[4,128,128]{2,1,0:T(8,128)(2,1)}), bf16[32,128,128]{2,1,0:T(8,128)(2,1)}) %all-gather.48.cloned.1.call-update) | async-done | bytes 1048592 | tf_op jit(solution)/shard_map/all_gather | solution.py:14
  711.1 8.7 %while.50 = (s32[]{:T(128)}, f32[4,128,128]{2,1,0:T(8,128)S(1)}, f32[4,128]{1,0:T(4,128)S(1)}, s32[]{:T(128)}, bf16[8,4,128,128]{3,2,1,0:T(8,128)(2,1)}, /*index...) while((s32[]{:T(128)}, f32[4,128,128]{2,1,0:T(8,128)S(1)}, f32[4,128]{1,0:T(4,128)S(1)}, ...), condition=%wide.region_23.24_spmd.clone, body=%wide.region_22.23_spmd.clone.sunk | while | flops 264196 | bytes 660595 | solution.py:31
  711.1 1.1 add_select_fusion.16
  717.6 1.0 add_select_fusion.16
  718.7 1.0 add_select_fusion.16
  722.3 39.8 %all-gather.50.cloned.1.call-done = bf16[1,512,2048]{2,1,0:T(8,128)(2,1)} async-done(((bf16[1,512,256]{2,1,0:T(8,128)(2,1)}), bf16[1,512,2048]{2,1,0:T(8,128)(2,1)}) %all-gather.50.cloned.1.call-update) | async-done | bytes 2097168 | tf_op jit(solution)/shard_map/all_gather | solution.py:101
  762.1 4.2 convolution_convert_fusion
  766.3 29.5 %reduce-scatter.8.cloned.1.call-done = bf16[512,512]{1,0:T(8,128)(2,1)} async-done(((bf16[512,2048]{1,0:T(8,128)(2,1)}), bf16[512,512]{1,0:T(8,128)(2,1)}) %reduce-scatter.8.cloned.1.call-update) | async-done | bytes 524304 | tf_op jit(solution)/shard_map/reduce_scatter | solution.py:104
  795.8 2.0 add_convert_fusion
  (149 shorter events, 27.2 us)
Async XLA Ops:
  6.5 27.7 %all-gather.28.cloned.1.call-start = ((), (), s32[]{:S(2)}) async-start(), calls=%async_computation.3 | async-start | bytes 2621440 | tf_op jit(solution)/shard_map/all_gather | solution.py:56
  7.3 3.3 copy-start.12
  7.3 127.9 %all-gather.34.cloned.1.call-start = ((), (), s32[]{:S(2)}) async-start(), calls=%async_computation.9 | async-start | bytes 7077888 | tf_op jit(solution)/shard_map/all_gather | solution.py:62
  10.5 176.4 %all-gather.36.cloned.1.call-start = ((), (), s32[]{:S(2)}) async-start(), calls=%async_computation.10 | async-start | bytes 1179648 | tf_op jit(solution)/shard_map/all_gather | solution.py:14
  34.2 100.9 %copy-start.3 = (bf16[512,2048]{1,0:T(8,128)(2,1)S(1)}, bf16[512,2048]{1,0:T(8,128)(2,1)}, u32[]{:S(2)}) copy-start(bf16[512,2048]{1,0:T(8,128)(2,1)} %all-gather.28.cloned.1.call-done) | copy-start | bytes 6291460
  147.3 4.0 copy-start.13
  148.3 89.6 %all-gather.38.cloned.1.call-start = ((), (), s32[]{:S(2)}) async-start(), calls=%async_computation.11 | async-start | bytes 2359296 | tf_op jit(solution)/shard_map/all_gather | solution.py:101
  150.4 121.2 %reduce-scatter.4.cloned.1.call-start = ((), (), s32[]{:S(2)}) async-start(), calls=%async_computation.4 | async-start | bytes 2621440 | tf_op jit(solution)/shard_map/reduce_scatter | solution.py:104
  169.3 2.6 copy-start.6
  186.9 9.6 %copy-start.7 = (pred[512,512]{0,1:T(8,128)(4,1)S(1)}, pred[512,512]{0,1:T(8,128)(4,1)}, u32[]{:S(2)}) copy-start(pred[512,512]{0,1:T(8,128)(4,1)} %iota_compare_fusion) | copy-start | bytes 786436
  195.6 1.7 copy-start.15
  242.1 29.5 %copy-start.2 = (bf16[512,512]{1,0:T(8,128)(2,1)S(1)}, bf16[512,512]{1,0:T(8,128)(2,1)}, u32[]{:S(2)}) copy-start(bf16[512,512]{1,0:T(8,128)(2,1)} %param.12) | copy-start | bytes 1572868
  242.1 54.2 %all-gather.30.cloned.1.call-start = ((), (), s32[]{:S(2)}) async-start(), calls=%async_computation.5 | async-start | bytes 2621440 | tf_op jit(solution)/shard_map/all_gather | solution.py:56
  273.6 123.6 %all-gather.40.cloned.1.call-start = ((), (), s32[]{:S(2)}) async-start(), calls=%async_computation.12 | async-start | bytes 7077888 | tf_op jit(solution)/shard_map/all_gather | solution.py:62
  274.4 174.6 %all-gather.42.cloned.1.call-start = ((), (), s32[]{:S(2)}) async-start(), calls=%async_computation.13 | async-start | bytes 1179648 | tf_op jit(solution)/shard_map/all_gather | solution.py:14
  296.3 100.9 %copy-start.5 = (bf16[512,2048]{1,0:T(8,128)(2,1)S(1)}, bf16[512,2048]{1,0:T(8,128)(2,1)}, u32[]{:S(2)}) copy-start(bf16[512,2048]{1,0:T(8,128)(2,1)} %all-gather.30.cloned.1.call-done) | copy-start | bytes 6291460
  410.4 89.7 %all-gather.44.cloned.1.call-start = ((), (), s32[]{:S(2)}) async-start(), calls=%async_computation.14 | async-start | bytes 2359296 | tf_op jit(solution)/shard_map/all_gather | solution.py:101
  411.2 122.7 %reduce-scatter.6.cloned.1.call-start = ((), (), s32[]{:S(2)}) async-start(), calls=%async_computation.6 | async-start | bytes 2621440 | tf_op jit(solution)/shard_map/reduce_scatter | solution.py:104
  429.2 2.6 copy-start.8
  449.0 9.6 %copy-start.9 = (pred[512,512]{0,1:T(8,128)(4,1)S(1)}, pred[512,512]{0,1:T(8,128)(4,1)}, u32[]{:S(2)}) copy-start(pred[512,512]{0,1:T(8,128)(4,1)} %iota_compare_fusion) | copy-start | bytes 786436
  457.7 1.7 copy-start.16
  504.3 29.5 %copy-start.1 = (bf16[512,512]{1,0:T(8,128)(2,1)S(1)}, bf16[512,512]{1,0:T(8,128)(2,1)}, u32[]{:S(2)}) copy-start(bf16[512,512]{1,0:T(8,128)(2,1)} %add_convert_fusion.2) | copy-start | bytes 1572868
  504.3 54.2 %all-gather.32.cloned.1.call-start = ((), (), s32[]{:S(2)}) async-start(), calls=%async_computation.7 | async-start | bytes 2621440 | tf_op jit(solution)/shard_map/all_gather | solution.py:56
  535.8 123.5 %all-gather.46.cloned.1.call-start = ((), (), s32[]{:S(2)}) async-start(), calls=%async_computation.15 | async-start | bytes 7077888 | tf_op jit(solution)/shard_map/all_gather | solution.py:62
  536.4 174.7 %all-gather.48.cloned.1.call-start = ((), (), s32[]{:S(2)}) async-start(), calls=%async_computation.16 | async-start | bytes 1179648 | tf_op jit(solution)/shard_map/all_gather | solution.py:14
  558.5 100.8 %copy-start.4 = (bf16[512,2048]{1,0:T(8,128)(2,1)S(1)}, bf16[512,2048]{1,0:T(8,128)(2,1)}, u32[]{:S(2)}) copy-start(bf16[512,2048]{1,0:T(8,128)(2,1)} %all-gather.32.cloned.1.call-done) | copy-start | bytes 6291460
  672.5 89.6 %all-gather.50.cloned.1.call-start = ((), (), s32[]{:S(2)}) async-start(), calls=%async_computation.17 | async-start | bytes 2359296 | tf_op jit(solution)/shard_map/all_gather | solution.py:101
  673.1 122.7 %reduce-scatter.8.cloned.1.call-start = ((), (), s32[]{:S(2)}) async-start(), calls=%async_computation.8 | async-start | bytes 2621440 | tf_op jit(solution)/shard_map/reduce_scatter | solution.py:104
  691.1 2.6 copy-start.10
  711.1 9.6 %copy-start.11 = (pred[512,512]{0,1:T(8,128)(4,1)S(1)}, pred[512,512]{0,1:T(8,128)(4,1)}, u32[]{:S(2)}) copy-start(pred[512,512]{0,1:T(8,128)(4,1)} %iota_compare_fusion) | copy-start | bytes 786436
  719.8 1.7 copy-start.14
  766.3 29.5 %copy-start = (bf16[512,512]{1,0:T(8,128)(2,1)S(1)}, bf16[512,512]{1,0:T(8,128)(2,1)}, u32[]{:S(2)}) copy-start(bf16[512,512]{1,0:T(8,128)(2,1)} %add_convert_fusion.1) | copy-start | bytes 1572868
Sparse Core Ops, SparseCore 0:
  8.9 25.2 all-gather.27
  36.4 98.6 all-gather.33
  148.4 38.4 all-gather.35
  188.8 49.0 all-gather.37
  242.2 29.3 reduce-scatter.3
  273.7 22.5 all-gather.29
  298.5 98.6 all-gather.39
  410.5 38.3 all-gather.41
  451.0 49.0 all-gather.43
  504.5 29.3 reduce-scatter.5
  535.9 22.5 all-gather.31
  560.6 98.6 all-gather.45
  672.6 38.4 all-gather.47
  713.0 49.0 all-gather.49
  766.4 29.3 reduce-scatter.7
where the time goes:
time: 806 us; the launch traced here: 804 us
  waiting for transfers between devices  618 us (77%)
  matrix products  62 us (8%)
  blocking collectives  53.2 us (7%)
  other arithmetic  41.7 us (5%)
  local copies, waits for them, and re-layouts  14.5 us (2%)
  between operations  13.8 us (2%)
    all_gather x3, waiting for transfers between devices, local(): lax.all_gather(qkv_weight[layer_index], 'seq', axis=0, tiled=True)  296 us
    all_gather x3, waiting for transfers between devices, local(): lax.all_gather(out_weight[layer_index], 'seq', axis=1, tiled=True)  120 us
    reduce_scatter x3, waiting for transfers between devices, local(): lax.psum_scatter(terms.astype(jnp.bfloat16), 'grp', scatter_dimension=1,...  88.4 us
    all_gather x3, waiting for transfers between devices, local(): gathered = lax.all_gather(stream, 'grp', axis=1, tiled=True)  67.3 us
    all_gather x3, blocking collectives, prefix(): lax.all_gather(part.astype(kind), axis)  53.2 us
    all_gather x3, waiting for transfers between devices, prefix(): lax.all_gather(part.astype(kind), axis)  43.3 us
    select_n x48, other arithmetic, step(): return jax.tree.map(lambda a, b: jnp.where(reached, a, b), new, before)  25.5 us
    dot_general x3, matrix products, local(): jnp.dot(normed, lax.all_gather(qkv_weight[layer_index], 'seq', axis=0, ti...  22.3 us
  transfers between devices with their start and end apart: 15, of which 15 were waited for; matrix products, arithmetic and copies ran while one was open for 7% of the time, Pallas kernels for 0%

commit v1 on v0

--- a/solution.py
+++ b/solution.py
@@ -3,6 +3,7 @@
 import jax.numpy as jnp
 from jax import lax
 from jax.sharding import PartitionSpec as P
+from jax.lax import axis_index, axis_size, ppermute
 
 stabilizer = 2.0
 highest = lax.Precision.HIGHEST
@@ -53,7 +54,21 @@
     stream = hidden
     causal_mask = jnp.arange(token_rows)[:, None] >= jnp.arange(token_rows)[None, :]
     for layer_index in range(layer_count):
-        gathered = lax.all_gather(stream, "grp", axis=1, tiled=True)
+
+        def edit_group_up(mine, ax_name):
+            n_shards = axis_size(ax_name)
+            x_now = sorted(((src_i, (src_i + 1) % n_shards) for src_i in range(n_shards)))
+            mixed_arr = mine
+            fields = [mixed_arr]
+            for p in [*range(1, n_shards)]:
+                mixed_arr = ppermute(mixed_arr, ax_name, x_now)
+                fields.insert(0, mixed_arr)
+            f_next = jnp.concatenate(fields, 1)
+            s_next = axis_index(ax_name) + 1
+            raw_out = jnp.roll(f_next, s_next * mine.shape[1], 1)
+            return raw_out
+
+        gathered = edit_group_up(stream, ax_name="grp")
         wide = gathered.astype(jnp.float32)
         inverse_rms = lax.rsqrt(jnp.mean(wide * wide, axis=-1, keepdims=True) + 1e-05)
         normed = (wide * inverse_rms * norm_gain[layer_index][None, :]).astype(jnp.bfloat16)

time: 806 us -> 742 us (0.921)
  waiting for transfers between devices: 618 us -> 525 us
  other arithmetic: 41.7 us -> 50.6 us
  matrix products: 62 us -> 70.2 us
    all_gather x3, waiting for transfers between devices: 296 us -> 205 us  [local(): lax.all_gather(qkv_weight[layer_index], 'seq', axis=0, tiled=True)]
    ppermute x0 -> x9, waiting for transfers between devices: none -> 76.9 us  [edit_group_up(): mixed_arr = ppermute(mixed_arr, ax_name, x_now)]
    all_gather x3 -> x0, waiting for transfers between devices: 67.3 us -> none  [local(): gathered = lax.all_gather(stream, 'grp', axis=1, tiled=True)]
    reduce_sum x3, other arithmetic: 6.67 us -> 17.3 us  [local(): jnp.mean(wide * wide, axis=-1, keepdims=True) + 1e-05]
  transfers between devices with their start and end apart: 15 -> 21, of which waited for: 15 -> 21; matrix products, arithmetic and copies ran while one was open for 7% -> 11% of each run, Pallas kernels for 0% -> 0%
where the time goes in v1:
time: 742 us; the launch traced here: 735 us
  waiting for transfers between devices  525 us (71%)
  matrix products  70.2 us (9%)
  blocking collectives  53.6 us (7%)
  other arithmetic  50.6 us (7%)
  local copies, waits for them, and re-layouts  18.8 us (3%)
  between operations  14.3 us (2%)
    all_gather x3, waiting for transfers between devices, local(): lax.all_gather(qkv_weight[layer_index], 'seq', axis=0, tiled=True)  205 us
    all_gather x3, waiting for transfers between devices, local(): lax.all_gather(out_weight[layer_index], 'seq', axis=1, tiled=True)  118 us
    reduce_scatter x3, waiting for transfers between devices, local(): lax.psum_scatter(terms.astype(jnp.bfloat16), 'grp', scatter_dimension=1,...  86.9 us
    ppermute x9, waiting for transfers between devices, edit_group_up(): mixed_arr = ppermute(mixed_arr, ax_name, x_now)  76.9 us
    all_gather x3, blocking collectives, prefix(): lax.all_gather(part.astype(kind), axis)  53.6 us
    all_gather x3, waiting for transfers between devices, prefix(): lax.all_gather(part.astype(kind), axis)  36.5 us
    select_n x48, other arithmetic, step(): return jax.tree.map(lambda a, b: jnp.where(reached, a, b), new, before)  25.4 us
    dot_general x3, matrix products, local(): jnp.dot(normed, lax.all_gather(qkv_weight[layer_index], 'seq', axis=0, ti...  22.3 us
  transfers between devices with their start and end apart: 21, of which 21 were waited for; matrix products, arithmetic and copies ran while one was open for 11% of the time, Pallas kernels for 0%

profile of v1, /device:TPU:0, one launch (start us, length us, event | category | flops | bytes accessed | tf_op | source)
XLA Modules:
  0.0 735.1 jit_solution(9751079724951482856)
XLA Ops:
  6.5 3.1 fusion.156
  10.3 8.8 %collective-permute-done = bf16[512,512]{1,0:T(8,128)(2,1)S(1)} collective-permute-done((bf16[512,512]{1,0:T(8,128)(2,1)S(1)}, bf16[512,512]{1,0:T(8,128)(2,1)S(1)}, u32[]{:S(2)}, u32[]{:S(2)}) %collective-permute-start) | collective-permute-done | bytes 524320 | tf_op jit(solution)/shard_map/ppermute | solution.py:64
  19.1 8.6 %collective-permute-done.1 = bf16[512,512]{1,0:T(8,128)(2,1)S(1)} collective-permute-done((bf16[512,512]{1,0:T(8,128)(2,1)S(1)}, bf16[512,512]{1,0:T(8,128)(2,1)S(1)}, u32[]{:S(2)}, u32[]{:S(2)}) %collective-permute-start.1) | collective-permute-done | bytes 524320 | tf_op jit(solution)/shard_map/ppermute | solution.py:64
  28.5 7.9 %collective-permute-done.2 = bf16[512,512]{1,0:T(8,128)(2,1)} collective-permute-done((bf16[512,512]{1,0:T(8,128)(2,1)S(1)}, bf16[512,512]{1,0:T(8,128)(2,1)}, u32[]{:S(2)}, u32[]{:S(2)}) %collective-permute-start.2) | collective-permute-done | bytes 524320 | tf_op jit(solution)/shard_map/ppermute | solution.py:64
  36.4 5.9 fusion.6
  42.3 68.9 %all-gather.25.cloned.1.call-done = bf16[1,2048,1536]{2,1,0:T(8,128)(2,1)} async-done(((bf16[1,256,1536]{2,1,0:T(8,128)(2,1)}), bf16[1,2048,1536]{2,1,0:T(8,128)(2,1)}) %all-gather.25.cloned.1.call-update) | async-done | bytes 6291472 | tf_op jit(solution)/shard_map/all_gather | solution.py:77
  111.3 7.4 %fusion.15 = bf16[512,1536]{1,0:T(8,128)(2,1)} fusion(bf16[1,2048,1536]{2,1,0:T(8,128)(2,1)} %all-gather.25.cloned.1.call-done, bf16[512,2048]{1,0:T(8,128)(2,1)S(1)} %get-tuple-element.446, f32[2048]{0:T(1024)S(1)} %bitcast.326, f32[512]{0:T(512)S(1)} %add_rsqrt_fusion.2), kind=kOutput, calls=%fused_computation.57 | convolution fusion | flops 3226206208 | bytes 9971712 | tf_op jit(solution)/shard_map/dot_general | solution.py:75
  118.7 1.7 copy.46
  121.2 2.3 fusion.163
  124.5 2.0 fusion.160
  127.4 18.0 %all-gather.12 = bf16[8,4,128]{2,1,0:T(4,128)(2,1)S(1)} all-gather(bf16[1,4,128]{2,1,0:T(4,128)(2,1)S(1)} %bitcast.327), channel_id=4, replica_groups=mesh['seq'=8,'grp'=4] {'seq'}, dimensions={0}, use_global_device_ids=true | all-gather | bytes 9216 | tf_op jit(solution)/shard_map/all_gather | solution.py:15
  146.1 2.2 fusion.98
  148.3 3.1 select_reduce_fusion.2
  151.4 11.7 %all-gather.27.cloned.1.call-done = bf16[32,128,128]{2,1,0:T(8,128)(2,1)} async-done(((bf16[4,128,128]{2,1,0:T(8,128)(2,1)}), bf16[32,128,128]{2,1,0:T(8,128)(2,1)}) %all-gather.27.cloned.1.call-update) | async-done | bytes 1048592 | tf_op jit(solution)/shard_map/all_gather | solution.py:15
  163.1 8.6 %while.48 = (s32[]{:T(128)}, f32[4,128,128]{2,1,0:T(8,128)S(1)}, f32[4,128]{1,0:T(4,128)S(1)}, s32[]{:T(128)}, bf16[8,4,128,128]{3,2,1,0:T(8,128)(2,1)}, /*index...) while((s32[]{:T(128)}, f32[4,128,128]{2,1,0:T(8,128)S(1)}, f32[4,128]{1,0:T(4,128)S(1)}, ...), condition=%wide.region_5.7_spmd.clone, body=%wide.region_4.6_spmd.clone.sunk | while | flops 264196 | bytes 660595 | solution.py:32
  164.1 1.0 add_select_fusion.12
  165.2 1.0 add_select_fusion.12
  167.4 1.0 add_select_fusion.12
  170.6 1.0 add_select_fusion.12
  172.6 2.2 multiply_reduce_fusion.2
  175.0 39.2 %all-gather.29.cloned.1.call-done = bf16[1,512,2048]{2,1,0:T(8,128)(2,1)} async-done(((bf16[1,512,256]{2,1,0:T(8,128)(2,1)}), bf16[1,512,2048]{2,1,0:T(8,128)(2,1)}) %all-gather.29.cloned.1.call-update) | async-done | bytes 2097168 | tf_op jit(solution)/shard_map/all_gather | solution.py:116
  214.2 4.3 convolution_convert_fusion.2
  219.1 28.9 %reduce-scatter.4.cloned.1.call-done = bf16[512,512]{1,0:T(8,128)(2,1)} async-done(((bf16[512,2048]{1,0:T(8,128)(2,1)}), bf16[512,512]{1,0:T(8,128)(2,1)}) %reduce-scatter.4.cloned.1.call-update) | async-done | bytes 524304 | tf_op jit(solution)/shard_map/reduce_scatter | solution.py:119
  248.0 1.2 add_convert_fusion.2
  249.2 8.6 %collective-permute-done.3 = bf16[512,512]{1,0:T(8,128)(2,1)S(1)} collective-permute-done((bf16[512,512]{1,0:T(8,128)(2,1)S(1)}, bf16[512,512]{1,0:T(8,128)(2,1)S(1)}, u32[]{:S(2)}, u32[]{:S(2)}) %collective-permute-start.3) | collective-permute-done | bytes 524320 | tf_op jit(solution)/shard_map/ppermute | solution.py:64
  257.8 8.6 %collective-permute-done.4 = bf16[512,512]{1,0:T(8,128)(2,1)S(1)} collective-permute-done((bf16[512,512]{1,0:T(8,128)(2,1)S(1)}, bf16[512,512]{1,0:T(8,128)(2,1)S(1)}, u32[]{:S(2)}, u32[]{:S(2)}) %collective-permute-start.4) | collective-permute-done | bytes 524320 | tf_op jit(solution)/shard_map/ppermute | solution.py:64
  266.9 8.6 %collective-permute-done.5 = bf16[512,512]{1,0:T(8,128)(2,1)S(1)} collective-permute-done((bf16[512,512]{1,0:T(8,128)(2,1)S(1)}, bf16[512,512]{1,0:T(8,128)(2,1)S(1)}, u32[]{:S(2)}, u32[]{:S(2)}) %collective-permute-start.5) | collective-permute-done | bytes 524320 | tf_op jit(solution)/shard_map/ppermute | solution.py:64
  275.5 5.7 fusion.9
  281.3 67.5 %all-gather.31.cloned.1.call-done = bf16[1,2048,1536]{2,1,0:T(8,128)(2,1)} async-done(((bf16[1,256,1536]{2,1,0:T(8,128)(2,1)}), bf16[1,2048,1536]{2,1,0:T(8,128)(2,1)}) %all-gather.31.cloned.1.call-update) | async-done | bytes 6291472 | tf_op jit(solution)/shard_map/all_gather | solution.py:77
  348.8 7.4 %fusion.18 = bf16[512,1536]{1,0:T(8,128)(2,1)} fusion(bf16[1,2048,1536]{2,1,0:T(8,128)(2,1)} %all-gather.31.cloned.1.call-done, bf16[512,2048]{1,0:T(8,128)(2,1)S(1)} %get-tuple-element.444, f32[2048]{0:T(1024)S(1)} %bitcast.325, f32[512]{0:T(512)S(1)} %add_rsqrt_fusion.1), kind=kOutput, calls=%fused_computation.58 | convolution fusion | flops 3226206208 | bytes 9971712 | tf_op jit(solution)/shard_map/dot_general | solution.py:75
  356.2 1.7 copy.54
  359.4 2.3 fusion.164
  364.4 17.7 %all-gather.13 = bf16[8,4,128]{2,1,0:T(4,128)(2,1)S(1)} all-gather(bf16[1,4,128]{2,1,0:T(4,128)(2,1)S(1)} %bitcast.329), channel_id=8, replica_groups=mesh['seq'=8,'grp'=4] {'seq'}, dimensions={0}, use_global_device_ids=true | all-gather | bytes 9216 | tf_op jit(solution)/shard_map/all_gather | solution.py:15
  382.1 1.3 copy.92
  383.8 2.2 fusion.96
  386.0 3.4 select_reduce_fusion.1
  389.4 12.7 %all-gather.33.cloned.1.call-done = bf16[32,128,128]{2,1,0:T(8,128)(2,1)} async-done(((bf16[4,128,128]{2,1,0:T(8,128)(2,1)}), bf16[32,128,128]{2,1,0:T(8,128)(2,1)}) %all-gather.33.cloned.1.call-update) | async-done | bytes 1048592 | tf_op jit(solution)/shard_map/all_gather | solution.py:15
  402.1 8.6 %while.49 = (s32[]{:T(128)}, f32[4,128,128]{2,1,0:T(8,128)S(1)}, f32[4,128]{1,0:T(4,128)S(1)}, s32[]{:T(128)}, bf16[8,4,128,128]{3,2,1,0:T(8,128)(2,1)}, /*index...) while((s32[]{:T(128)}, f32[4,128,128]{2,1,0:T(8,128)S(1)}, f32[4,128]{1,0:T(4,128)S(1)}, ...), condition=%wide.region_14.16_spmd.clone, body=%wide.region_13.15_spmd.clone.sunk | while | flops 264196 | bytes 660595 | solution.py:32
  409.7 1.0 add_select_fusion.14
  411.6 2.2 multiply_reduce_fusion.1
  414.0 39.2 %all-gather.35.cloned.1.call-done = bf16[1,512,2048]{2,1,0:T(8,128)(2,1)} async-done(((bf16[1,512,256]{2,1,0:T(8,128)(2,1)}), bf16[1,512,2048]{2,1,0:T(8,128)(2,1)}) %all-gather.35.cloned.1.call-update) | async-done | bytes 2097168 | tf_op jit(solution)/shard_map/all_gather | solution.py:116
  453.2 4.2 convolution_convert_fusion.1
  458.4 28.5 %reduce-scatter.6.cloned.1.call-done = bf16[512,512]{1,0:T(8,128)(2,1)} async-done(((bf16[512,2048]{1,0:T(8,128)(2,1)}), bf16[512,512]{1,0:T(8,128)(2,1)}) %reduce-scatter.6.cloned.1.call-update) | async-done | bytes 524304 | tf_op jit(solution)/shard_map/reduce_scatter | solution.py:119
  486.9 1.2 add_convert_fusion.1
  488.2 8.6 %collective-permute-done.6 = bf16[512,512]{1,0:T(8,128)(2,1)S(1)} collective-permute-done((bf16[512,512]{1,0:T(8,128)(2,1)S(1)}, bf16[512,512]{1,0:T(8,128)(2,1)S(1)}, u32[]{:S(2)}, u32[]{:S(2)}) %collective-permute-start.6) | collective-permute-done | bytes 524320 | tf_op jit(solution)/shard_map/ppermute | solution.py:64
  496.8 8.6 %collective-permute-done.7 = bf16[512,512]{1,0:T(8,128)(2,1)S(1)} collective-permute-done((bf16[512,512]{1,0:T(8,128)(2,1)S(1)}, bf16[512,512]{1,0:T(8,128)(2,1)S(1)}, u32[]{:S(2)}, u32[]{:S(2)}) %collective-permute-start.7) | collective-permute-done | bytes 524320 | tf_op jit(solution)/shard_map/ppermute | solution.py:64
  505.4 8.6 %collective-permute-done.8 = bf16[512,512]{1,0:T(8,128)(2,1)S(1)} collective-permute-done((bf16[512,512]{1,0:T(8,128)(2,1)S(1)}, bf16[512,512]{1,0:T(8,128)(2,1)S(1)}, u32[]{:S(2)}, u32[]{:S(2)}) %collective-permute-start.8) | collective-permute-done | bytes 524320 | tf_op jit(solution)/shard_map/ppermute | solution.py:64
  514.0 5.7 fusion.12
  519.7 68.1 %all-gather.37.cloned.1.call-done = bf16[1,2048,1536]{2,1,0:T(8,128)(2,1)} async-done(((bf16[1,256,1536]{2,1,0:T(8,128)(2,1)}), bf16[1,2048,1536]{2,1,0:T(8,128)(2,1)}) %all-gather.37.cloned.1.call-update) | async-done | bytes 6291472 | tf_op jit(solution)/shard_map/all_gather | solution.py:77
  587.9 7.4 %fusion.21 = bf16[512,1536]{1,0:T(8,128)(2,1)} fusion(bf16[1,2048,1536]{2,1,0:T(8,128)(2,1)} %all-gather.37.cloned.1.call-done, bf16[512,2048]{1,0:T(8,128)(2,1)S(1)} %get-tuple-element.442, f32[2048]{0:T(1024)S(1)} %bitcast.324, f32[512]{0:T(512)S(1)} %add_rsqrt_fusion), kind=kOutput, calls=%fused_computation.59 | convolution fusion | flops 3226206208 | bytes 9971712 | tf_op jit(solution)/shard_map/dot_general | solution.py:75
  595.3 1.7 copy.62
  598.5 2.3 fusion.165
  603.5 17.9 %all-gather.14 = bf16[8,4,128]{2,1,0:T(4,128)(2,1)S(1)} all-gather(bf16[1,4,128]{2,1,0:T(4,128)(2,1)S(1)} %bitcast.328), channel_id=12, replica_groups=mesh['seq'=8,'grp'=4] {'seq'}, dimensions={0}, use_global_device_ids=true | all-gather | bytes 9216 | tf_op jit(solution)/shard_map/all_gather | solution.py:15
  621.4 1.3 copy.95
  623.5 2.4 fusion.94
  625.9 3.2 select_reduce_fusion
  629.1 12.1 %all-gather.39.cloned.1.call-done = bf16[32,128,128]{2,1,0:T(8,128)(2,1)} async-done(((bf16[4,128,128]{2,1,0:T(8,128)(2,1)}), bf16[32,128,128]{2,1,0:T(8,128)(2,1)}) %all-gather.39.cloned.1.call-update) | async-done | bytes 1048592 | tf_op jit(solution)/shard_map/all_gather | solution.py:15
  641.2 8.6 %while.50 = (s32[]{:T(128)}, f32[4,128,128]{2,1,0:T(8,128)S(1)}, f32[4,128]{1,0:T(4,128)S(1)}, s32[]{:T(128)}, bf16[8,4,128,128]{3,2,1,0:T(8,128)(2,1)}, /*index...) while((s32[]{:T(128)}, f32[4,128,128]{2,1,0:T(8,128)S(1)}, f32[4,128]{1,0:T(4,128)S(1)}, ...), condition=%wide.region_23.25_spmd.clone, body=%wide.region_22.24_spmd.clone.sunk | while | flops 264196 | bytes 660595 | solution.py:32
  648.8 1.0 add_select_fusion.16
  650.7 2.2 multiply_reduce_fusion
  653.1 39.3 %all-gather.41.cloned.1.call-done = bf16[1,512,2048]{2,1,0:T(8,128)(2,1)} async-done(((bf16[1,512,256]{2,1,0:T(8,128)(2,1)}), bf16[1,512,2048]{2,1,0:T(8,128)(2,1)}) %all-gather.41.cloned.1.call-update) | async-done | bytes 2097168 | tf_op jit(solution)/shard_map/all_gather | solution.py:116
  692.3 4.2 convolution_convert_fusion
  696.6 29.5 %reduce-scatter.8.cloned.1.call-done = bf16[512,512]{1,0:T(8,128)(2,1)} async-done(((bf16[512,2048]{1,0:T(8,128)(2,1)}), bf16[512,512]{1,0:T(8,128)(2,1)}) %reduce-scatter.8.cloned.1.call-update) | async-done | bytes 524304 | tf_op jit(solution)/shard_map/reduce_scatter | solution.py:119
  726.0 2.0 add_convert_fusion
  (144 shorter events, 38.7 us)
Async XLA Ops:
  6.5 3.2 copy-start.1
  6.5 21.2 %copy-start.8 = (f32[3,2048]{1,0:T(4,128)S(1)}, f32[3,2048]{1,0:T(4,128)}, u32[]{:S(2)}) copy-start(f32[3,2048]{1,0:T(4,128)} %param.18) | copy-start | bytes 73732
  6.5 104.7 %all-gather.25.cloned.1.call-start = ((), (), s32[]{:S(2)}) async-start(), calls=%async_computation.6 | async-start | bytes 7077888 | tf_op jit(solution)/shard_map/all_gather | solution.py:77
  9.7 153.3 %all-gather.27.cloned.1.call-start = ((), (), s32[]{:S(2)}) async-start(), calls=%async_computation.7 | async-start | bytes 1179648 | tf_op jit(solution)/shard_map/all_gather | solution.py:15
  9.8 9.3 %collective-permute-start = (bf16[512,512]{1,0:T(8,128)(2,1)S(1)}, bf16[512,512]{1,0:T(8,128)(2,1)S(1)}, u32[]{:S(2)}, u32[]{:S(2)}) collective-permute-start(bf16[512,512]{1,0:T(8,128)(2,1)S(1)} %copy-done.1), channel_id=1, source_target_pairs={{0,1},{1,2},{2,3},{3,0},{4,5},{5,6},{6,7},{7,4},{8,9},{9,10},{10,1... | collective-permute-start | bytes 1572872 | tf_op jit(solution)/shard_map/ppermute | solution.py:64
  19.1 8.6 %collective-permute-start.1 = (bf16[512,512]{1,0:T(8,128)(2,1)S(1)}, bf16[512,512]{1,0:T(8,128)(2,1)S(1)}, u32[]{:S(2)}, u32[]{:S(2)}) collective-permute-start(bf16[512,512]{1,0:T(8,128)(2,1)S(1)} %collective-permute-done), channel_id=1, source_target_pairs={{0,1},{1,2},{2,3},{3,0},{4,5},{5,6},{6,7},{7,4},{8,9},{9,10},{10,1... | collective-permute-start | bytes 1572872 | tf_op jit(solution)/shard_map/ppermute | solution.py:64
  27.7 0.8 copy-start.5
  27.7 8.7 %collective-permute-start.2 = (bf16[512,512]{1,0:T(8,128)(2,1)S(1)}, bf16[512,512]{1,0:T(8,128)(2,1)}, u32[]{:S(2)}, u32[]{:S(2)}) collective-permute-start(bf16[512,512]{1,0:T(8,128)(2,1)S(1)} %collective-permute-done.1), channel_id=1, source_target_pairs={{0,1},{1,2},{2,3},{3,0},{4,5},{5,6},{6,7},{7,4},{8,9},{9,10},{10,1... | collective-permute-start | bytes 1572872 | tf_op jit(solution)/shard_map/ppermute | solution.py:64
  120.4 7.0 copy-start.9
  124.4 89.8 %all-gather.29.cloned.1.call-start = ((), (), s32[]{:S(2)}) async-start(), calls=%async_computation.8 | async-start | bytes 2359296 | tf_op jit(solution)/shard_map/all_gather | solution.py:116
  126.5 121.4 %reduce-scatter.4.cloned.1.call-start = ((), (), s32[]{:S(2)}) async-start(), calls=%async_computation.3 | async-start | bytes 2621440 | tf_op jit(solution)/shard_map/reduce_scatter | solution.py:119
  148.3 24.3 %copy-start.6 = (pred[512,512]{0,1:T(8,128)(4,1)S(1)}, pred[512,512]{0,1:T(8,128)(4,1)}, u32[]{:S(2)}) copy-start(pred[512,512]{0,1:T(8,128)(4,1)} %iota_compare_fusion) | copy-start | bytes 786436
  214.2 33.8 %copy-start.2 = (bf16[512,512]{1,0:T(8,128)(2,1)S(1)}, bf16[512,512]{1,0:T(8,128)(2,1)}, u32[]{:S(2)}) copy-start(bf16[512,512]{1,0:T(8,128)(2,1)} %param.14) | copy-start | bytes 1572868
  218.5 130.3 %all-gather.31.cloned.1.call-start = ((), (), s32[]{:S(2)}) async-start(), calls=%async_computation.9 | async-start | bytes 7077888 | tf_op jit(solution)/shard_map/all_gather | solution.py:77
  219.1 183.0 %all-gather.33.cloned.1.call-start = ((), (), s32[]{:S(2)}) async-start(), calls=%async_computation.10 | async-start | bytes 1179648 | tf_op jit(solution)/shard_map/all_gather | solution.py:15
  249.2 8.7 %collective-permute-start.3 = (bf16[512,512]{1,0:T(8,128)(2,1)S(1)}, bf16[512,512]{1,0:T(8,128)(2,1)S(1)}, u32[]{:S(2)}, u32[]{:S(2)}) collective-permute-start(bf16[512,512]{1,0:T(8,128)(2,1)S(1)} %add_convert_fusion.2), channel_id=1, source_target_pairs={{0,1},{1,2},{2,3},{3,0},{4,5},{5,6},{6,7},{7,4},{8,9},{9,10},{10,1... | collective-permute-start | bytes 1572872 | tf_op jit(solution)/shard_map/ppermute | solution.py:64
  257.8 8.6 %collective-permute-start.4 = (bf16[512,512]{1,0:T(8,128)(2,1)S(1)}, bf16[512,512]{1,0:T(8,128)(2,1)S(1)}, u32[]{:S(2)}, u32[]{:S(2)}) collective-permute-start(bf16[512,512]{1,0:T(8,128)(2,1)S(1)} %collective-permute-done.3), channel_id=1, source_target_pairs={{0,1},{1,2},{2,3},{3,0},{4,5},{5,6},{6,7},{7,4},{8,9},{9,10},{10,1... | collective-permute-start | bytes 1572872 | tf_op jit(solution)/shard_map/ppermute | solution.py:64
  266.4 9.1 %collective-permute-start.5 = (bf16[512,512]{1,0:T(8,128)(2,1)S(1)}, bf16[512,512]{1,0:T(8,128)(2,1)S(1)}, u32[]{:S(2)}, u32[]{:S(2)}) collective-permute-start(bf16[512,512]{1,0:T(8,128)(2,1)S(1)} %collective-permute-done.4), channel_id=1, source_target_pairs={{0,1},{1,2},{2,3},{3,0},{4,5},{5,6},{6,7},{7,4},{8,9},{9,10},{10,1... | collective-permute-start | bytes 1572872 | tf_op jit(solution)/shard_map/ppermute | solution.py:64
  361.7 0.8 copy-start.4
  363.6 89.7 %all-gather.35.cloned.1.call-start = ((), (), s32[]{:S(2)}) async-start(), calls=%async_computation.11 | async-start | bytes 2359296 | tf_op jit(solution)/shard_map/all_gather | solution.py:116
  364.3 122.6 %reduce-scatter.6.cloned.1.call-start = ((), (), s32[]{:S(2)}) async-start(), calls=%async_computation.4 | async-start | bytes 2621440 | tf_op jit(solution)/shard_map/reduce_scatter | solution.py:119
  386.0 25.7 %copy-start.7 = (pred[512,512]{0,1:T(8,128)(4,1)S(1)}, pred[512,512]{0,1:T(8,128)(4,1)}, u32[]{:S(2)}) copy-start(pred[512,512]{0,1:T(8,128)(4,1)} %iota_compare_fusion) | copy-start | bytes 786436
  457.5 130.4 %all-gather.37.cloned.1.call-start = ((), (), s32[]{:S(2)}) async-start(), calls=%async_computation.12 | async-start | bytes 7077888 | tf_op jit(solution)/shard_map/all_gather | solution.py:77
  458.2 183.0 %all-gather.39.cloned.1.call-start = ((), (), s32[]{:S(2)}) async-start(), calls=%async_computation.13 | async-start | bytes 1179648 | tf_op jit(solution)/shard_map/all_gather | solution.py:15
  488.1 8.7 %collective-permute-start.6 = (bf16[512,512]{1,0:T(8,128)(2,1)S(1)}, bf16[512,512]{1,0:T(8,128)(2,1)S(1)}, u32[]{:S(2)}, u32[]{:S(2)}) collective-permute-start(bf16[512,512]{1,0:T(8,128)(2,1)S(1)} %add_convert_fusion.1), channel_id=1, source_target_pairs={{0,1},{1,2},{2,3},{3,0},{4,5},{5,6},{6,7},{7,4},{8,9},{9,10},{10,1... | collective-permute-start | bytes 1572872 | tf_op jit(solution)/shard_map/ppermute | solution.py:64
  496.8 8.6 %collective-permute-start.7 = (bf16[512,512]{1,0:T(8,128)(2,1)S(1)}, bf16[512,512]{1,0:T(8,128)(2,1)S(1)}, u32[]{:S(2)}, u32[]{:S(2)}) collective-permute-start(bf16[512,512]{1,0:T(8,128)(2,1)S(1)} %collective-permute-done.6), channel_id=1, source_target_pairs={{0,1},{1,2},{2,3},{3,0},{4,5},{5,6},{6,7},{7,4},{8,9},{9,10},{10,1... | collective-permute-start | bytes 1572872 | tf_op jit(solution)/shard_map/ppermute | solution.py:64
  505.4 8.6 %collective-permute-start.8 = (bf16[512,512]{1,0:T(8,128)(2,1)S(1)}, bf16[512,512]{1,0:T(8,128)(2,1)S(1)}, u32[]{:S(2)}, u32[]{:S(2)}) collective-permute-start(bf16[512,512]{1,0:T(8,128)(2,1)S(1)} %collective-permute-done.7), channel_id=1, source_target_pairs={{0,1},{1,2},{2,3},{3,0},{4,5},{5,6},{6,7},{7,4},{8,9},{9,10},{10,1... | collective-permute-start | bytes 1572872 | tf_op jit(solution)/shard_map/ppermute | solution.py:64
  600.8 0.8 copy-start.3
  602.7 89.7 %all-gather.41.cloned.1.call-start = ((), (), s32[]{:S(2)}) async-start(), calls=%async_computation.14 | async-start | bytes 2359296 | tf_op jit(solution)/shard_map/all_gather | solution.py:116
  603.4 122.7 %reduce-scatter.8.cloned.1.call-start = ((), (), s32[]{:S(2)}) async-start(), calls=%async_computation.5 | async-start | bytes 2621440 | tf_op jit(solution)/shard_map/reduce_scatter | solution.py:119
  622.7 0.8 copy-start
Sparse Core Ops, SparseCore 0:
  9.8 101.4 all-gather.24
  124.6 38.4 all-gather.26
  165.1 49.0 all-gather.28
  218.6 29.3 reduce-scatter.3
  250.0 98.6 all-gather.30
  363.7 38.3 all-gather.32
  404.1 49.0 all-gather.34
  457.6 29.3 reduce-scatter.5
  489.1 98.6 all-gather.36
  602.8 38.3 all-gather.38
  643.3 49.0 all-gather.40
  696.7 29.3 reduce-scatter.7
